TPU v7x, 32 devices: a whole 2x2x4 slice. The times are simulated.
32 devices in a mesh: gx: 8 (over z, y), gy: 4 (over x, core).
Axes of the slice: x: 2, y: 2, z: 4, core: 2. Of those that a mesh axis runs over, the one named last changes fastest.
Arguments:
- liquid_starting_warmth: float32 [32, 64, 1024], P('gx', 'gy'), may hold values from -6 to 6
- liquid_spreading_ratios: float32 [32, 64, 1024], P('gx', 'gy'), may hold values from 0.02 to 0.12
- liquid_advective_ratios: float32 [3, 32, 64, 1024], P(None, 'gx', 'gy'), may hold values from -0.08 to 0.08
- liquid_refresh_flags: int32 [32, 64, 8], P('gx', 'gy'), may hold values 0 or 1
- wall_starting_warmth: float32 [32, 64, 1024], P('gx', 'gy'), may hold values from -6 to 6
- wall_thermal_capacity: float32 [32, 64, 1024], P('gx', 'gy'), may hold values from 0.5 to 2
- thermal_conductance: float32 [32, 64, 1024], P('gx', 'gy'), may hold values from 0.5 to 15
- wall_energy_output: float32 [32, 64, 1024], P('gx', 'gy'), may hold values from -36 to 36
- coupling_partner_lookup: int32 [32, 64], P('gx', 'gy'), may hold values from 0 to 63, each once within a row
Outputs:
- fluid_after: float32 [32, 64, 1024], P('gx', 'gy')
- solid_after: float32 [32, 64, 1024], P('gx', 'gy')
Inputs may be any that keep to these rules, and one draw needn't show every extreme that they name: For each first index, the row of coupling_partner_lookup holds every number of 0 to 63 once.
All inputs are finite; a program needn't handle non-finite values. No bound on the sum of `liquid_refresh_flags` on one device may be relied on, other than what follows from the above.
Results may differ from a plain program's by a relative error of at most 0.00023.
Values sent between devices are 32-bit elements; how exact they have to be, the bound alone decides.
A program may use at most 64 MiB of HBM per device.

v0:
```python
import jax
import jax.numpy as jnp
from jax import lax
from jax.sharding import PartitionSpec as P

SUBSTEPS = 4
ITERS = 4
ZB = 128


def padded_2(cells, sides, width):
    for axis, dim in sides:
        count = lax.axis_size(axis)
        ends = count - 1
        head = lax.slice_in_dim(cells, 0, width, axis=dim)
        tail = lax.slice_in_dim(cells, cells.shape[dim] - width, cells.shape[dim], axis=dim)
        cells = jnp.concatenate(
            [
                lax.ppermute(tail, axis, [(i, (i + 1) % count) for i in range(ends)]),
                cells,
                lax.ppermute(head, axis, [((i + 1) % count, i) for i in range(ends)]),
            ],
            axis=dim,
        )
    return cells


def advance(current_estimate, padded, ghost_row, diffusion, velocity, active_cells):
    below = jnp.concatenate([ghost_row[:, :, None], current_estimate[:, :, :-1]], axis=2)
    above = jnp.concatenate(
        [current_estimate[:, :, 1:], jnp.zeros_like(current_estimate[:, :, :1])], axis=2
    )
    couples = (
        (padded[:-2, 1:-1], padded[2:, 1:-1]),
        (padded[1:-1, :-2], padded[1:-1, 2:]),
        (below, above),
    )
    spread = -6.0 * current_estimate
    carried = jnp.zeros_like(current_estimate)
    for component in range(3):
        behind, ahead = couples[component]
        spread = spread + behind + ahead
        flow_speed = velocity[component]
        carried = (
            carried
            + jnp.maximum(flow_speed, 0.0) * (current_estimate - behind)
            + jnp.minimum(flow_speed, 0.0) * (ahead - current_estimate)
        )
    return current_estimate + active_cells * (diffusion * spread - carried)


def neighbours(field, padded):
    below = jnp.concatenate([jnp.zeros_like(field[:, :, :1]), field[:, :, :-1]], axis=2)
    above = jnp.concatenate([field[:, :, 1:], jnp.zeros_like(field[:, :, :1])], axis=2)
    return (padded[:-2, 1:-1], padded[2:, 1:-1], padded[1:-1, :-2], padded[1:-1, 2:], below, above)


def thermal_flow_operator(field, padded_field, thermal_conductance, bordered_conductance, capacity):
    accumulated = capacity * field
    for near_value, near_cond in zip(
        neighbours(field, padded_field), neighbours(thermal_conductance, bordered_conductance)
    ):
        accumulated = accumulated + 0.5 * (thermal_conductance + near_cond) * (field - near_value)
    return accumulated


def diagonal_of(thermal_conductance, bordered_conductance, capacity):
    accumulated = capacity
    for near_cond in neighbours(thermal_conductance, bordered_conductance):
        accumulated = accumulated + 0.5 * (thermal_conductance + near_cond)
    return accumulated


def local(
    liquid_starting_warmth,
    liquid_spreading_ratios,
    liquid_advective_ratios,
    liquid_refresh_flags,
    wall_starting_warmth,
    wall_thermal_capacity,
    thermal_conductance,
    wall_energy_output,
    coupling_partner_lookup,
):
    local_cols = coupling_partner_lookup.shape[1]
    topmost_layers = lax.all_gather(wall_starting_warmth[:, :, -1], "gy", axis=1, tiled=True)
    positions = jnp.arange(topmost_layers.shape[1], dtype=jnp.int32)
    picks = coupling_partner_lookup[:, :, None] == positions[None, None, :]
    ghost_row = jnp.sum(jnp.where(picks, topmost_layers[:, None, :], 0.0), axis=2)
    active_cells = jnp.repeat(liquid_refresh_flags.astype(jnp.float32), ZB, axis=2)
    padded_fluid, bordered_wall_warmth, bordered_conductance = (
        padded_2(liquid_starting_warmth, (("gx", 0), ("gy", 1)), 1),
        padded_2(wall_starting_warmth, (("gx", 0), ("gy", 1)), 1),
        padded_2(thermal_conductance, (("gx", 0), ("gy", 1)), 1),
    )
    current_estimate = liquid_starting_warmth
    padded = padded_fluid
    flux_sum = jnp.zeros_like(ghost_row)
    for substep in range(SUBSTEPS):
        flux_sum = flux_sum + (current_estimate[:, :, 0] - ghost_row)
        if substep > 0:
            padded = padded_2(current_estimate, (("gx", 0), ("gy", 1)), 1)
        current_estimate = advance(
            current_estimate,
            padded,
            ghost_row,
            liquid_spreading_ratios,
            liquid_advective_ratios,
            active_cells,
        )
    flux_mean = flux_sum / SUBSTEPS
    map_wide = lax.all_gather(coupling_partner_lookup, "gy", axis=1, tiled=True)
    flux_wide = lax.all_gather(flux_mean, "gy", axis=1, tiled=True)
    own_cols = lax.axis_index("gy") * local_cols + jnp.arange(local_cols, dtype=jnp.int32)
    owners = map_wide[:, None, :] == own_cols[None, :, None]
    arrived = jnp.sum(jnp.where(owners, flux_wide[:, None, :], 0.0), axis=2)
    equation_source_term = wall_thermal_capacity * wall_starting_warmth + wall_energy_output
    equation_source_term = equation_source_term.at[:, :, -1].add(arrived)
    diagonal = diagonal_of(thermal_conductance, bordered_conductance, wall_thermal_capacity)

    def apply_stiffness_matrix(field, padded_field):
        return thermal_flow_operator(
            field, padded_field, thermal_conductance, bordered_conductance, wall_thermal_capacity
        )

    def rimmed(field):
        return padded_2(field, (("gx", 0), ("gy", 1)), 1)

    converged_warmth = wall_starting_warmth
    leftover_error = equation_source_term - apply_stiffness_matrix(
        converged_warmth, bordered_wall_warmth
    )
    scaled = leftover_error / diagonal

    def paired(residual_now, scaled_now, image_now):
        return lax.psum(
            (jnp.sum(residual_now * scaled_now), jnp.sum(scaled_now * image_now)), ("gx", "gy")
        )

    image = apply_stiffness_matrix(scaled, rimmed(scaled))
    inner_rz, curvature = paired(leftover_error, scaled, image)
    descent_length = inner_rz / curvature
    search_heading = scaled
    image_dir = image
    for iteration in range(ITERS):
        converged_warmth = converged_warmth + descent_length * search_heading
        leftover_error = leftover_error - descent_length * image_dir
        if iteration + 1 < ITERS:
            scaled = leftover_error / diagonal
            image = apply_stiffness_matrix(scaled, rimmed(scaled))
            inner_next, curvature = paired(leftover_error, scaled, image)
            ratio = inner_next / inner_rz
            descent_length = inner_next / (curvature - ratio * inner_next / descent_length)
            search_heading = scaled + ratio * search_heading
            image_dir = image + ratio * image_dir
            inner_rz = inner_next
    return (current_estimate, converged_warmth)


def solution(mesh):
    return jax.shard_map(
        local,
        mesh=mesh,
        in_specs=(
            P("gx", "gy", None),
            P("gx", "gy", None),
            P(None, "gx", "gy", None),
            P("gx", "gy", None),
            P("gx", "gy", None),
            P("gx", "gy", None),
            P("gx", "gy", None),
            P("gx", "gy", None),
            P("gx", "gy"),
        ),
        out_specs=(P("gx", "gy", None), P("gx", "gy", None)),
        check_vma=False,
    )
```

profile of v0, /device:TPU:0, one launch (start us, length us, event | category | flops | bytes accessed | tf_op | source)
XLA Modules:
  0.0 360.6 jit_solution(3652510717344675397)
XLA Ops:
  1.6 4.9 %collective-permute-start = (f32[1,16,1024]{2,1,0:T(8,128)S(1)}, f32[1,16,1024]{2,1,0:T(8,128)S(1)}, u32[]{:S(2)}, u32[]{:S(2)}) collective-permute-start(f32[1,16,1024]{2,1,0:T(8,128)S(1)} %get-tuple-element.112), channel_id=1, source_target_pairs={{0,4},{4,8},{8,12},{12,16},{16,20},{20,24},{24,28},{1,5},{5,9},{9,... | collective-permute-start | bytes 196616 | tf_op jit(solution)/shard_map/ppermute | solution.py:19
  9.3 5.2 %collective-permute-start.17 = (f32[1,16,1024]{2,1,0:T(8,128)S(1)}, f32[1,16,1024]{2,1,0:T(8,128)S(1)}, u32[]{:S(2)}, u32[]{:S(2)}) collective-permute-start(f32[1,16,1024]{2,1,0:T(8,128)S(1)} %get-tuple-element.91), channel_id=1, source_target_pairs={{0,4},{4,8},{8,12},{12,16},{16,20},{20,24},{24,28},{1,5},{5,9},{9,... | collective-permute-start | bytes 196616 | tf_op jit(solution)/shard_map/ppermute | solution.py:19
  14.5 4.8 %collective-permute-start.16 = (f32[1,16,1024]{2,1,0:T(8,128)S(1)}, f32[1,16,1024]{2,1,0:T(8,128)S(1)}, u32[]{:S(2)}, u32[]{:S(2)}) collective-permute-start(f32[1,16,1024]{2,1,0:T(8,128)S(1)} %get-tuple-element.96), channel_id=1, source_target_pairs={{0,4},{4,8},{8,12},{12,16},{16,20},{20,24},{24,28},{1,5},{5,9},{9,... | collective-permute-start | bytes 196616 | tf_op jit(solution)/shard_map/ppermute | solution.py:19
  22.1 5.3 %all-gather.1 = s32[4,16,4]{1,2,0:T(4,128)S(1)} all-gather(s32[1,16,4]{1,2,0:T(4,128)S(1)} %bitcast.80), channel_id=1, replica_groups=mesh['gx'=8,'gy'=4] {'gy'}, dimensions={0}, use_global_device_ids=true | all-gather | bytes 1280 | tf_op jit(solution)/shard_map/all_gather | solution.py:112
  27.6 5.4 %all-gather = f32[4,64,1]{2,1,0:T(8,128)S(1)} all-gather(f32[4,16,1]{2,1,0:T(8,128)S(1)} %slice.433), channel_id=2, replica_groups=mesh['gx'=8,'gy'=4] {'gy'}, dimensions={1}, use_global_device_ids=true | all-gather | bytes 1280 | tf_op jit(solution)/shard_map/all_gather | solution.py:86
  34.9 4.9 %collective-permute-done.18 = f32[1,16,1024]{2,1,0:T(8,128)S(1)} collective-permute-done((f32[1,16,1024]{2,1,0:T(8,128)S(1)}, f32[1,16,1024]{2,1,0:T(8,128)S(1)}, u32[]{:S(2)}, u32[]{:S(2)}) %collective-permute-start.18) | collective-permute-done | bytes 65568 | tf_op jit(solution)/shard_map/ppermute | solution.py:21
  53.2 4.3 %collective-permute-start.4 = (f32[1,16,1024]{2,1,0:T(8,128)S(1)}, f32[1,16,1024]{2,1,0:T(8,128)S(1)}, u32[]{:S(2)}, u32[]{:S(2)}) collective-permute-start(f32[1,16,1024]{2,1,0:T(8,128)S(1)} %get-tuple-element.108), channel_id=1, source_target_pairs={{0,4},{4,8},{8,12},{12,16},{16,20},{20,24},{24,28},{1,5},{5,9},{9,... | collective-permute-start | bytes 196616 | tf_op jit(solution)/shard_map/ppermute | solution.py:19
  59.4 4.5 %collective-permute-done.5 = f32[1,16,1024]{2,1,0:T(8,128)S(1)} collective-permute-done((f32[1,16,1024]{2,1,0:T(8,128)S(1)}, f32[1,16,1024]{2,1,0:T(8,128)S(1)}, u32[]{:S(2)}, u32[]{:S(2)}) %collective-permute-start.5) | collective-permute-done | bytes 65568 | tf_op jit(solution)/shard_map/ppermute | solution.py:21
  70.4 3.4 collective-permute-start.8
  75.7 4.3 %collective-permute-done.9 = f32[1,16,1024]{2,1,0:T(8,128)S(1)} collective-permute-done((f32[1,16,1024]{2,1,0:T(8,128)S(1)}, f32[1,16,1024]{2,1,0:T(8,128)S(1)}, u32[]{:S(2)}, u32[]{:S(2)}) %collective-permute-start.9) | collective-permute-done | bytes 65568 | tf_op jit(solution)/shard_map/ppermute | solution.py:21
  87.6 6.6 %all-gather.2 = f32[4,16,4]{1,2,0:T(4,128)S(1)} all-gather(f32[1,16,4]{1,2,0:T(4,128)S(1)} %multiply_bitcast_fusion), channel_id=1, replica_groups=mesh['gx'=8,'gy'=4] {'gy'}, dimensions={0}, use_global_device_ids=true | all-gather | bytes 1280 | tf_op jit(solution)/shard_map/all_gather | solution.py:113
  98.5 4.3 %collective-permute-start.24 = (f32[1,16,1024]{2,1,0:T(8,128)S(1)}, f32[1,16,1024]{2,1,0:T(8,128)S(1)}, u32[]{:S(2)}, u32[]{:S(2)}) collective-permute-start(f32[1,16,1024]{2,1,0:T(8,128)S(1)} %get-tuple-element.84), channel_id=1, source_target_pairs={{0,4},{4,8},{8,12},{12,16},{16,20},{20,24},{24,28},{1,5},{5,9},{9,... | collective-permute-start | bytes 196616 | tf_op jit(solution)/shard_map/ppermute | solution.py:19
  105.0 4.0 %collective-permute-done.25 = f32[1,16,1024]{2,1,0:T(8,128)S(1)} collective-permute-done((f32[1,16,1024]{2,1,0:T(8,128)S(1)}, f32[1,16,1024]{2,1,0:T(8,128)S(1)}, u32[]{:S(2)}, u32[]{:S(2)}) %collective-permute-start.25) | collective-permute-done | bytes 65568 | tf_op jit(solution)/shard_map/ppermute | solution.py:21
  111.8 3.4 collective-permute-done.27
  117.0 41.0 %all-reduce.19 = (f32[]{:T(128)}, f32[]{:T(128)}) all-reduce(f32[]{:T(128)} %get-tuple-element.27, f32[]{:T(128)} %get-tuple-element.26), channel_id=1, replica_groups=mesh['gx'=8,'gy'=4] {'gx','gy'}, use_global_device_ids=true, to_apply=%region_3.4 | all-reduce | flops 2 | bytes 16 | tf_op jit(solution)/shard_map/psum | solution.py:136
  160.4 4.4 %collective-permute-start.28 = (f32[1,16,1024]{2,1,0:T(8,128)S(1)}, f32[1,16,1024]{2,1,0:T(8,128)S(1)}, u32[]{:S(2)}, u32[]{:S(2)}) collective-permute-start(f32[1,16,1024]{2,1,0:T(8,128)S(1)} %get-tuple-element.80), channel_id=1, source_target_pairs={{0,4},{4,8},{8,12},{12,16},{16,20},{20,24},{24,28},{1,5},{5,9},{9,... | collective-permute-start | bytes 196616 | tf_op jit(solution)/shard_map/ppermute | solution.py:19
  166.7 5.2 %collective-permute-start.12 = (f32[1,16,1024]{2,1,0:T(8,128)}, f32[1,16,1024]{2,1,0:T(8,128)}, u32[]{:S(2)}, u32[]{:S(2)}) collective-permute-start(f32[1,16,1024]{2,1,0:T(8,128)} %get-tuple-element.100), channel_id=1, source_target_pairs={{0,4},{4,8},{8,12},{12,16},{16,20},{20,24},{24,28},{1,5},{5,9},{9,... | collective-permute-start | bytes 196616 | tf_op jit(solution)/shard_map/ppermute | solution.py:19
  180.8 42.0 %all-reduce.18 = (f32[]{:T(128)}, f32[]{:T(128)}) all-reduce(f32[]{:T(128)} %get-tuple-element.25, f32[]{:T(128)} %get-tuple-element.24), channel_id=1, replica_groups=mesh['gx'=8,'gy'=4] {'gx','gy'}, use_global_device_ids=true, to_apply=%region_7.8 | all-reduce | flops 2 | bytes 16 | tf_op jit(solution)/shard_map/psum | solution.py:136
  228.3 4.4 %collective-permute-start.32 = (f32[1,16,1024]{2,1,0:T(8,128)S(1)}, f32[1,16,1024]{2,1,0:T(8,128)S(1)}, u32[]{:S(2)}, u32[]{:S(2)}) collective-permute-start(f32[1,16,1024]{2,1,0:T(8,128)S(1)} %get-tuple-element.76), channel_id=1, source_target_pairs={{0,4},{4,8},{8,12},{12,16},{16,20},{20,24},{24,28},{1,5},{5,9},{9,... | collective-permute-start | bytes 196616 | tf_op jit(solution)/shard_map/ppermute | solution.py:19
  238.9 4.5 %collective-permute-start.34 = (f32[6,1,1024]{2,1,0:T(1,128)S(1)}, f32[6,1,1024]{2,1,0:T(1,128)S(1)}, u32[]{:S(2)}, u32[]{:S(2)}) collective-permute-start(f32[6,1,1024]{2,1,0:T(1,128)S(1)} %get-tuple-element.54), channel_id=1, source_target_pairs={{0,1},{1,2},{2,3},{4,5},{5,6},{6,7},{8,9},{9,10},{10,11},{12,13},{... | collective-permute-start | bytes 73736 | tf_op jit(solution)/shard_map/ppermute | solution.py:19
  249.6 41.4 %all-reduce.17 = (f32[]{:T(128)}, f32[]{:T(128)}) all-reduce(f32[]{:T(128)} %get-tuple-element.23, f32[]{:T(128)} %get-tuple-element.22), channel_id=1, replica_groups=mesh['gx'=8,'gy'=4] {'gx','gy'}, use_global_device_ids=true, to_apply=%region_11.12 | all-reduce | flops 2 | bytes 16 | tf_op jit(solution)/shard_map/psum | solution.py:136
  296.8 4.6 %collective-permute-start.36 = (f32[1,16,1024]{2,1,0:T(8,128)S(1)}, f32[1,16,1024]{2,1,0:T(8,128)S(1)}, u32[]{:S(2)}, u32[]{:S(2)}) collective-permute-start(f32[1,16,1024]{2,1,0:T(8,128)S(1)} %get-tuple-element.74), channel_id=1, source_target_pairs={{0,4},{4,8},{8,12},{12,16},{16,20},{20,24},{24,28},{1,5},{5,9},{9,... | collective-permute-start | bytes 196616 | tf_op jit(solution)/shard_map/ppermute | solution.py:19
  310.5 3.3 collective-permute-done.39
  314.8 41.4 %all-reduce.16 = (f32[]{:T(128)}, f32[]{:T(128)}) all-reduce(f32[]{:T(128)} %get-tuple-element.36, f32[]{:T(128)} %fusion.6), channel_id=1, replica_groups=mesh['gx'=8,'gy'=4] {'gx','gy'}, use_global_device_ids=true, to_apply=%region_15.16 | all-reduce | flops 2 | bytes 16 | tf_op jit(solution)/shard_map/psum | solution.py:136
  (207 shorter events, 88.5 us)
Async XLA Ops:
  1.6 39.6 %collective-permute-start = (f32[1,16,1024]{2,1,0:T(8,128)S(1)}, f32[1,16,1024]{2,1,0:T(8,128)S(1)}, u32[]{:S(2)}, u32[]{:S(2)}) collective-permute-start(f32[1,16,1024]{2,1,0:T(8,128)S(1)} %get-tuple-element.112), channel_id=1, source_target_pairs={{0,4},{4,8},{8,12},{12,16},{16,20},{20,24},{24,28},{1,5},{5,9},{9,... | collective-permute-start | bytes 196616 | tf_op jit(solution)/shard_map/ppermute | solution.py:19
  6.5 37.8 %collective-permute-start.1 = (f32[1,16,1024]{2,1,0:T(8,128)S(1)}, f32[1,16,1024]{2,1,0:T(8,128)S(1)}, u32[]{:S(2)}, u32[]{:S(2)}) collective-permute-start(f32[1,16,1024]{2,1,0:T(8,128)S(1)} %get-tuple-element.113), channel_id=1, source_target_pairs={{4,0},{8,4},{12,8},{16,12},{20,16},{24,20},{28,24},{5,1},{9,5},{13... | collective-permute-start | bytes 196616 | tf_op jit(solution)/shard_map/ppermute | solution.py:21
  8.0 41.0 %collective-permute-start.19 = (f32[1,16,1024]{2,1,0:T(8,128)S(1)}, f32[1,16,1024]{2,1,0:T(8,128)S(1)}, u32[]{:S(2)}, u32[]{:S(2)}) collective-permute-start(f32[1,16,1024]{2,1,0:T(8,128)S(1)} %get-tuple-element.90), channel_id=1, source_target_pairs={{4,0},{8,4},{12,8},{16,12},{20,16},{24,20},{28,24},{5,1},{9,5},{13... | collective-permute-start | bytes 196616 | tf_op jit(solution)/shard_map/ppermute | solution.py:21
  9.3 38.3 %collective-permute-start.17 = (f32[1,16,1024]{2,1,0:T(8,128)S(1)}, f32[1,16,1024]{2,1,0:T(8,128)S(1)}, u32[]{:S(2)}, u32[]{:S(2)}) collective-permute-start(f32[1,16,1024]{2,1,0:T(8,128)S(1)} %get-tuple-element.91), channel_id=1, source_target_pairs={{0,4},{4,8},{8,12},{12,16},{16,20},{20,24},{24,28},{1,5},{5,9},{9,... | collective-permute-start | bytes 196616 | tf_op jit(solution)/shard_map/ppermute | solution.py:19
  14.5 19.1 %collective-permute-start.16 = (f32[1,16,1024]{2,1,0:T(8,128)S(1)}, f32[1,16,1024]{2,1,0:T(8,128)S(1)}, u32[]{:S(2)}, u32[]{:S(2)}) collective-permute-start(f32[1,16,1024]{2,1,0:T(8,128)S(1)} %get-tuple-element.96), channel_id=1, source_target_pairs={{0,4},{4,8},{8,12},{12,16},{16,20},{20,24},{24,28},{1,5},{5,9},{9,... | collective-permute-start | bytes 196616 | tf_op jit(solution)/shard_map/ppermute | solution.py:19
  33.6 6.2 %collective-permute-start.18 = (f32[1,16,1024]{2,1,0:T(8,128)S(1)}, f32[1,16,1024]{2,1,0:T(8,128)S(1)}, u32[]{:S(2)}, u32[]{:S(2)}) collective-permute-start(f32[1,16,1024]{2,1,0:T(8,128)S(1)} %get-tuple-element.97), channel_id=1, source_target_pairs={{4,0},{8,4},{12,8},{16,12},{20,16},{24,20},{28,24},{5,1},{9,5},{13... | collective-permute-start | bytes 196616 | tf_op jit(solution)/shard_map/ppermute | solution.py:21
  39.9 55.1 %collective-permute-start.22 = (f32[6,1,1024]{2,1,0:T(1,128)S(1)}, f32[6,1,1024]{2,1,0:T(1,128)S(1)}, u32[]{:S(2)}, u32[]{:S(2)}) collective-permute-start(f32[6,1,1024]{2,1,0:T(1,128)S(1)} %get-tuple-element.60), channel_id=1, source_target_pairs={{1,0},{2,1},{3,2},{5,4},{6,5},{7,6},{9,8},{10,9},{11,10},{13,12},{... | collective-permute-start | bytes 73736 | tf_op jit(solution)/shard_map/ppermute | solution.py:21
  41.2 53.8 %collective-permute-start.20 = (f32[6,1,1024]{2,1,0:T(1,128)S(1)}, f32[6,1,1024]{2,1,0:T(1,128)S(1)}, u32[]{:S(2)}, u32[]{:S(2)}) collective-permute-start(f32[6,1,1024]{2,1,0:T(1,128)S(1)} %get-tuple-element.61), channel_id=1, source_target_pairs={{0,1},{1,2},{2,3},{4,5},{5,6},{6,7},{8,9},{9,10},{10,11},{12,13},{... | collective-permute-start | bytes 73736 | tf_op jit(solution)/shard_map/ppermute | solution.py:19
  44.4 8.3 %collective-permute-start.2 = (f32[6,1,1024]{2,1,0:T(1,128)S(1)}, f32[6,1,1024]{2,1,0:T(1,128)S(1)}, u32[]{:S(2)}, u32[]{:S(2)}) collective-permute-start(f32[6,1,1024]{2,1,0:T(1,128)S(1)} %get-tuple-element.70), channel_id=1, source_target_pairs={{0,1},{1,2},{2,3},{4,5},{5,6},{6,7},{8,9},{9,10},{10,11},{12,13},{... | collective-permute-start | bytes 73736 | tf_op jit(solution)/shard_map/ppermute | solution.py:19
  49.7 45.4 %collective-permute-start.21 = (f32[6,1,1024]{2,1,0:T(1,128)S(1)}, f32[6,1,1024]{2,1,0:T(1,128)S(1)}, u32[]{:S(2)}, u32[]{:S(2)}) collective-permute-start(f32[6,1,1024]{2,1,0:T(1,128)S(1)} %get-tuple-element.62), channel_id=1, source_target_pairs={{0,1},{1,2},{2,3},{4,5},{5,6},{6,7},{8,9},{9,10},{10,11},{12,13},{... | collective-permute-start | bytes 73736 | tf_op jit(solution)/shard_map/ppermute | solution.py:19
  53.2 6.2 %collective-permute-start.4 = (f32[1,16,1024]{2,1,0:T(8,128)S(1)}, f32[1,16,1024]{2,1,0:T(8,128)S(1)}, u32[]{:S(2)}, u32[]{:S(2)}) collective-permute-start(f32[1,16,1024]{2,1,0:T(8,128)S(1)} %get-tuple-element.108), channel_id=1, source_target_pairs={{0,4},{4,8},{8,12},{12,16},{16,20},{20,24},{24,28},{1,5},{5,9},{9,... | collective-permute-start | bytes 196616 | tf_op jit(solution)/shard_map/ppermute | solution.py:19
  57.5 6.4 %collective-permute-start.5 = (f32[1,16,1024]{2,1,0:T(8,128)S(1)}, f32[1,16,1024]{2,1,0:T(8,128)S(1)}, u32[]{:S(2)}, u32[]{:S(2)}) collective-permute-start(f32[1,16,1024]{2,1,0:T(8,128)S(1)} %get-tuple-element.109), channel_id=1, source_target_pairs={{4,0},{8,4},{12,8},{16,12},{20,16},{24,20},{28,24},{5,1},{9,5},{13... | collective-permute-start | bytes 196616 | tf_op jit(solution)/shard_map/ppermute | solution.py:21
  73.8 6.2 %collective-permute-start.9 = (f32[1,16,1024]{2,1,0:T(8,128)S(1)}, f32[1,16,1024]{2,1,0:T(8,128)S(1)}, u32[]{:S(2)}, u32[]{:S(2)}) collective-permute-start(f32[1,16,1024]{2,1,0:T(8,128)S(1)} %get-tuple-element.105), channel_id=1, source_target_pairs={{4,0},{8,4},{12,8},{16,12},{20,16},{24,20},{28,24},{5,1},{9,5},{13... | collective-permute-start | bytes 196616 | tf_op jit(solution)/shard_map/ppermute | solution.py:21
  84.4 10.6 %collective-permute-start.23 = (f32[6,1,1024]{2,1,0:T(1,128)S(1)}, f32[6,1,1024]{2,1,0:T(1,128)S(1)}, u32[]{:S(2)}, u32[]{:S(2)}) collective-permute-start(f32[6,1,1024]{2,1,0:T(1,128)S(1)} %get-tuple-element.63), channel_id=1, source_target_pairs={{1,0},{2,1},{3,2},{5,4},{6,5},{7,6},{9,8},{10,9},{11,10},{13,12},{... | collective-permute-start | bytes 73736 | tf_op jit(solution)/shard_map/ppermute | solution.py:21
  98.5 6.5 %collective-permute-start.24 = (f32[1,16,1024]{2,1,0:T(8,128)S(1)}, f32[1,16,1024]{2,1,0:T(8,128)S(1)}, u32[]{:S(2)}, u32[]{:S(2)}) collective-permute-start(f32[1,16,1024]{2,1,0:T(8,128)S(1)} %get-tuple-element.84), channel_id=1, source_target_pairs={{0,4},{4,8},{8,12},{12,16},{16,20},{20,24},{24,28},{1,5},{5,9},{9,... | collective-permute-start | bytes 196616 | tf_op jit(solution)/shard_map/ppermute | solution.py:19
  102.9 6.2 %collective-permute-start.25 = (f32[1,16,1024]{2,1,0:T(8,128)S(1)}, f32[1,16,1024]{2,1,0:T(8,128)S(1)}, u32[]{:S(2)}, u32[]{:S(2)}) collective-permute-start(f32[1,16,1024]{2,1,0:T(8,128)S(1)} %get-tuple-element.85), channel_id=1, source_target_pairs={{4,0},{8,4},{12,8},{16,12},{20,16},{24,20},{28,24},{5,1},{9,5},{13... | collective-permute-start | bytes 196616 | tf_op jit(solution)/shard_map/ppermute | solution.py:21
  160.4 12.8 %collective-permute-start.28 = (f32[1,16,1024]{2,1,0:T(8,128)S(1)}, f32[1,16,1024]{2,1,0:T(8,128)S(1)}, u32[]{:S(2)}, u32[]{:S(2)}) collective-permute-start(f32[1,16,1024]{2,1,0:T(8,128)S(1)} %get-tuple-element.80), channel_id=1, source_target_pairs={{0,4},{4,8},{8,12},{12,16},{16,20},{20,24},{24,28},{1,5},{5,9},{9,... | collective-permute-start | bytes 196616 | tf_op jit(solution)/shard_map/ppermute | solution.py:19
  164.8 8.4 %collective-permute-start.29 = (f32[1,16,1024]{2,1,0:T(8,128)S(1)}, f32[1,16,1024]{2,1,0:T(8,128)S(1)}, u32[]{:S(2)}, u32[]{:S(2)}) collective-permute-start(f32[1,16,1024]{2,1,0:T(8,128)S(1)} %get-tuple-element.81), channel_id=1, source_target_pairs={{4,0},{8,4},{12,8},{16,12},{20,16},{24,20},{28,24},{5,1},{9,5},{13... | collective-permute-start | bytes 196616 | tf_op jit(solution)/shard_map/ppermute | solution.py:21
  166.7 67.2 %collective-permute-start.12 = (f32[1,16,1024]{2,1,0:T(8,128)}, f32[1,16,1024]{2,1,0:T(8,128)}, u32[]{:S(2)}, u32[]{:S(2)}) collective-permute-start(f32[1,16,1024]{2,1,0:T(8,128)} %get-tuple-element.100), channel_id=1, source_target_pairs={{0,4},{4,8},{8,12},{12,16},{16,20},{20,24},{24,28},{1,5},{5,9},{9,... | collective-permute-start | bytes 196616 | tf_op jit(solution)/shard_map/ppermute | solution.py:19
  171.9 62.1 %collective-permute-start.13 = (f32[1,16,1024]{2,1,0:T(8,128)}, f32[1,16,1024]{2,1,0:T(8,128)}, u32[]{:S(2)}, u32[]{:S(2)}) collective-permute-start(f32[1,16,1024]{2,1,0:T(8,128)} %get-tuple-element.101), channel_id=1, source_target_pairs={{4,0},{8,4},{12,8},{16,12},{20,16},{24,20},{28,24},{5,1},{9,5},{13... | collective-permute-start | bytes 196616 | tf_op jit(solution)/shard_map/ppermute | solution.py:21
  228.3 10.4 %collective-permute-start.32 = (f32[1,16,1024]{2,1,0:T(8,128)S(1)}, f32[1,16,1024]{2,1,0:T(8,128)S(1)}, u32[]{:S(2)}, u32[]{:S(2)}) collective-permute-start(f32[1,16,1024]{2,1,0:T(8,128)S(1)} %get-tuple-element.76), channel_id=1, source_target_pairs={{0,4},{4,8},{8,12},{12,16},{16,20},{20,24},{24,28},{1,5},{5,9},{9,... | collective-permute-start | bytes 196616 | tf_op jit(solution)/shard_map/ppermute | solution.py:19
  235.5 67.2 %collective-permute-start.14 = (f32[6,1,1024]{2,1,0:T(1,128)}, f32[6,1,1024]{2,1,0:T(1,128)}, u32[]{:S(2)}, u32[]{:S(2)}) collective-permute-start(f32[6,1,1024]{2,1,0:T(1,128)} %get-tuple-element.64), channel_id=1, source_target_pairs={{0,1},{1,2},{2,3},{4,5},{5,6},{6,7},{8,9},{9,10},{10,11},{12,13},{... | collective-permute-start | bytes 73736 | tf_op jit(solution)/shard_map/ppermute | solution.py:19
  237.3 65.4 %collective-permute-start.15 = (f32[6,1,1024]{2,1,0:T(1,128)}, f32[6,1,1024]{2,1,0:T(1,128)}, u32[]{:S(2)}, u32[]{:S(2)}) collective-permute-start(f32[6,1,1024]{2,1,0:T(1,128)} %get-tuple-element.65), channel_id=1, source_target_pairs={{1,0},{2,1},{3,2},{5,4},{6,5},{7,6},{9,8},{10,9},{11,10},{13,12},{... | collective-permute-start | bytes 73736 | tf_op jit(solution)/shard_map/ppermute | solution.py:21
  296.8 7.9 %collective-permute-start.36 = (f32[1,16,1024]{2,1,0:T(8,128)S(1)}, f32[1,16,1024]{2,1,0:T(8,128)S(1)}, u32[]{:S(2)}, u32[]{:S(2)}) collective-permute-start(f32[1,16,1024]{2,1,0:T(8,128)S(1)} %get-tuple-element.74), channel_id=1, source_target_pairs={{0,4},{4,8},{8,12},{12,16},{16,20},{20,24},{24,28},{1,5},{5,9},{9,... | collective-permute-start | bytes 196616 | tf_op jit(solution)/shard_map/ppermute | solution.py:19
  (51 other events, 555.7 us)
where the time goes:
time: 363 us; the launch traced here: 361 us
  blocking collectives  183 us (50%)
  starting transfers between devices  96.6 us (27%)
  waiting for transfers between devices  38 us (10%)
  other arithmetic  19.5 us (5%)
  between operations  14.5 us (4%)
  local copies, waits for them, and re-layouts  8.88 us (2%)
    psum x4, blocking collectives, paired(): lax.psum((jnp.sum(residual_now * scaled_now), jnp.sum(scaled_now * image_...  166 us
    ppermute x20, starting transfers between devices, padded_2(): lax.ppermute(tail, axis, [(i, (i + 1) % count) for i in range(ends)])  70.2 us
    ppermute x20, waiting for transfers between devices, padded_2(): lax.ppermute(head, axis, [((i + 1) % count, i) for i in range(ends)])  37.1 us
    ppermute x20, starting transfers between devices, padded_2(): lax.ppermute(head, axis, [((i + 1) % count, i) for i in range(ends)])  26.3 us
  transfers between devices with their start and end apart: 40, of which 14 were waited for; matrix products, arithmetic and copies ran while one was open for 5% of the time, Pallas kernels for 0%

commit v1 on v0

--- a/solution.py
+++ b/solution.py
@@ -1,3 +1,4 @@
+import functools
 import jax
 import jax.numpy as jnp
 from jax import lax
@@ -6,6 +7,13 @@
 SUBSTEPS = 4
 ITERS = 4
 ZB = 128
+
+
+def turn_the_face(in_array, axis_tag, axis_key):
+    return lax.psum(lax.psum(in_array, axis_tag), axis_name=axis_key)
+
+
+prepare_node = functools.partial(turn_the_face, axis_tag="gy", axis_key="gx")
 
 
 def padded_2(cells, sides, width):
@@ -133,9 +141,7 @@
     scaled = leftover_error / diagonal
 
     def paired(residual_now, scaled_now, image_now):
-        return lax.psum(
-            (jnp.sum(residual_now * scaled_now), jnp.sum(scaled_now * image_now)), ("gx", "gy")
-        )
+        return prepare_node((jnp.sum(residual_now * scaled_now), jnp.sum(scaled_now * image_now)))
 
     image = apply_stiffness_matrix(scaled, rimmed(scaled))
     inner_rz, curvature = paired(leftover_error, scaled, image)

time: 363 us -> 310 us (0.85)
  blocking collectives: 183 us -> 133 us
  starting transfers between devices: 96.6 us -> 87.9 us
  local copies, waits for them, and re-layouts: 8.88 us -> 13.7 us
    psum x4 -> x8, blocking collectives: 166 us -> 115 us  [turn_the_face(): return lax.psum(lax.psum(in_array, axis_tag), axis_name=axis_key)]
    ppermute x20, starting transfers between devices: 70.2 us -> 61.6 us  [padded_2(): lax.ppermute(tail, axis, [(i, (i + 1) % count) for i in range(ends)])]
  transfers between devices with their start and end apart: 40 -> 40, of which waited for: 14 -> 14; matrix products, arithmetic and copies ran while one was open for 5% -> 7% of each run, Pallas kernels for 0% -> 0%
where the time goes in v1:
time: 310 us; the launch traced here: 308 us
  blocking collectives  133 us (43%)
  starting transfers between devices  87.9 us (28%)
  waiting for transfers between devices  38.8 us (13%)
  other arithmetic  19.9 us (6%)
  between operations  15.2 us (5%)
  local copies, waits for them, and re-layouts  13.7 us (4%)
    psum x8, blocking collectives, turn_the_face(): return lax.psum(lax.psum(in_array, axis_tag), axis_name=axis_key)  115 us
    ppermute x20, starting transfers between devices, padded_2(): lax.ppermute(tail, axis, [(i, (i + 1) % count) for i in range(ends)])  61.6 us
    ppermute x20, waiting for transfers between devices, padded_2(): lax.ppermute(head, axis, [((i + 1) % count, i) for i in range(ends)])  37.8 us
    ppermute x20, starting transfers between devices, padded_2(): lax.ppermute(head, axis, [((i + 1) % count, i) for i in range(ends)])  26.3 us
    all_gather x1, blocking collectives, local(): flux_wide = lax.all_gather(flux_mean, 'gy', axis=1, tiled=True)  6.63 us
  transfers between devices with their start and end apart: 40, of which 14 were waited for; matrix products, arithmetic and copies ran while one was open for 7% of the time, Pallas kernels for 0%

profile of v1, /device:TPU:0, one launch (start us, length us, event | category | flops | bytes accessed | tf_op | source)
XLA Modules:
  0.0 308.3 jit_solution(17066482543853057386)
XLA Ops:
  1.6 4.9 %collective-permute-start = (f32[1,16,1024]{2,1,0:T(8,128)S(1)}, f32[1,16,1024]{2,1,0:T(8,128)S(1)}, u32[]{:S(2)}, u32[]{:S(2)}) collective-permute-start(f32[1,16,1024]{2,1,0:T(8,128)S(1)} %get-tuple-element.120), channel_id=1, source_target_pairs={{0,4},{4,8},{8,12},{12,16},{16,20},{20,24},{24,28},{1,5},{5,9},{9,... | collective-permute-start | bytes 196616 | tf_op jit(solution)/shard_map/ppermute | solution.py:27
  9.9 5.2 %collective-permute-start.17 = (f32[1,16,1024]{2,1,0:T(8,128)S(1)}, f32[1,16,1024]{2,1,0:T(8,128)S(1)}, u32[]{:S(2)}, u32[]{:S(2)}) collective-permute-start(f32[1,16,1024]{2,1,0:T(8,128)S(1)} %get-tuple-element.99), channel_id=1, source_target_pairs={{0,4},{4,8},{8,12},{12,16},{16,20},{20,24},{24,28},{1,5},{5,9},{9,... | collective-permute-start | bytes 196616 | tf_op jit(solution)/shard_map/ppermute | solution.py:27
  15.1 4.8 %collective-permute-start.16 = (f32[1,16,1024]{2,1,0:T(8,128)S(1)}, f32[1,16,1024]{2,1,0:T(8,128)S(1)}, u32[]{:S(2)}, u32[]{:S(2)}) collective-permute-start(f32[1,16,1024]{2,1,0:T(8,128)S(1)} %get-tuple-element.104), channel_id=1, source_target_pairs={{0,4},{4,8},{8,12},{12,16},{16,20},{20,24},{24,28},{1,5},{5,9},{9,... | collective-permute-start | bytes 196616 | tf_op jit(solution)/shard_map/ppermute | solution.py:27
  23.3 5.3 %all-gather.1 = s32[4,16,4]{1,2,0:T(4,128)S(1)} all-gather(s32[1,16,4]{1,2,0:T(4,128)S(1)} %bitcast.80), channel_id=1, replica_groups=mesh['gx'=8,'gy'=4] {'gy'}, dimensions={0}, use_global_device_ids=true | all-gather | bytes 1280 | tf_op jit(solution)/shard_map/all_gather | solution.py:120
  29.3 5.4 %all-gather = f32[4,64,1]{2,1,0:T(8,128)S(1)} all-gather(f32[4,16,1]{2,1,0:T(8,128)S(1)} %slice.433), channel_id=2, replica_groups=mesh['gx'=8,'gy'=4] {'gy'}, dimensions={1}, use_global_device_ids=true | all-gather | bytes 1280 | tf_op jit(solution)/shard_map/all_gather | solution.py:94
  37.7 4.9 %collective-permute-done.18 = f32[1,16,1024]{2,1,0:T(8,128)S(1)} collective-permute-done((f32[1,16,1024]{2,1,0:T(8,128)S(1)}, f32[1,16,1024]{2,1,0:T(8,128)S(1)}, u32[]{:S(2)}, u32[]{:S(2)}) %collective-permute-start.18) | collective-permute-done | bytes 65568 | tf_op jit(solution)/shard_map/ppermute | solution.py:29
  57.3 4.3 %collective-permute-start.4 = (f32[1,16,1024]{2,1,0:T(8,128)S(1)}, f32[1,16,1024]{2,1,0:T(8,128)S(1)}, u32[]{:S(2)}, u32[]{:S(2)}) collective-permute-start(f32[1,16,1024]{2,1,0:T(8,128)S(1)} %get-tuple-element.116), channel_id=1, source_target_pairs={{0,4},{4,8},{8,12},{12,16},{16,20},{20,24},{24,28},{1,5},{5,9},{9,... | collective-permute-start | bytes 196616 | tf_op jit(solution)/shard_map/ppermute | solution.py:27
  63.5 4.5 %collective-permute-done.5 = f32[1,16,1024]{2,1,0:T(8,128)S(1)} collective-permute-done((f32[1,16,1024]{2,1,0:T(8,128)S(1)}, f32[1,16,1024]{2,1,0:T(8,128)S(1)}, u32[]{:S(2)}, u32[]{:S(2)}) %collective-permute-start.5) | collective-permute-done | bytes 65568 | tf_op jit(solution)/shard_map/ppermute | solution.py:29
  79.8 4.3 %collective-permute-done.9 = f32[1,16,1024]{2,1,0:T(8,128)S(1)} collective-permute-done((f32[1,16,1024]{2,1,0:T(8,128)S(1)}, f32[1,16,1024]{2,1,0:T(8,128)S(1)}, u32[]{:S(2)}, u32[]{:S(2)}) %collective-permute-start.9) | collective-permute-done | bytes 65568 | tf_op jit(solution)/shard_map/ppermute | solution.py:29
  92.2 6.6 %all-gather.2 = f32[4,16,4]{1,2,0:T(4,128)S(1)} all-gather(f32[1,16,4]{1,2,0:T(4,128)S(1)} %multiply_bitcast_fusion), channel_id=1, replica_groups=mesh['gx'=8,'gy'=4] {'gy'}, dimensions={0}, use_global_device_ids=true | all-gather | bytes 1280 | tf_op jit(solution)/shard_map/all_gather | solution.py:121
  103.9 4.3 %collective-permute-start.24 = (f32[1,16,1024]{2,1,0:T(8,128)S(1)}, f32[1,16,1024]{2,1,0:T(8,128)S(1)}, u32[]{:S(2)}, u32[]{:S(2)}) collective-permute-start(f32[1,16,1024]{2,1,0:T(8,128)S(1)} %get-tuple-element.92), channel_id=1, source_target_pairs={{0,4},{4,8},{8,12},{12,16},{16,20},{20,24},{24,28},{1,5},{5,9},{9,... | collective-permute-start | bytes 196616 | tf_op jit(solution)/shard_map/ppermute | solution.py:27
  110.4 4.0 %collective-permute-done.25 = f32[1,16,1024]{2,1,0:T(8,128)S(1)} collective-permute-done((f32[1,16,1024]{2,1,0:T(8,128)S(1)}, f32[1,16,1024]{2,1,0:T(8,128)S(1)}, u32[]{:S(2)}, u32[]{:S(2)}) %collective-permute-start.25) | collective-permute-done | bytes 65568 | tf_op jit(solution)/shard_map/ppermute | solution.py:29
  122.3 8.8 %all-reduce.23 = (f32[]{:T(128)}, f32[]{:T(128)}) all-reduce(f32[]{:T(128)} %get-tuple-element.27, f32[]{:T(128)} %get-tuple-element.26), channel_id=1, replica_groups=mesh['gx'=8,'gy'=4] {'gy'}, use_global_device_ids=true, to_apply=%region_3.4 | all-reduce | flops 2 | bytes 16 | tf_op jit(solution)/shard_map/psum | solution.py:13
  131.1 19.3 %all-reduce.19 = (f32[]{:T(128)}, f32[]{:T(128)}) all-reduce(f32[]{:T(128)} %get-tuple-element.42, f32[]{:T(128)} %get-tuple-element.43), channel_id=1, replica_groups=mesh['gx'=8,'gy'=4] {'gx'}, use_global_device_ids=true, to_apply=%region_4.5 | all-reduce | flops 2 | bytes 16 | tf_op jit(solution)/shard_map/psum | solution.py:13
  157.3 5.2 %collective-permute-start.12 = (f32[1,16,1024]{2,1,0:T(8,128)}, f32[1,16,1024]{2,1,0:T(8,128)}, u32[]{:S(2)}, u32[]{:S(2)}) collective-permute-start(f32[1,16,1024]{2,1,0:T(8,128)} %get-tuple-element.108), channel_id=1, source_target_pairs={{0,4},{4,8},{8,12},{12,16},{16,20},{20,24},{24,28},{1,5},{5,9},{9,... | collective-permute-start | bytes 196616 | tf_op jit(solution)/shard_map/ppermute | solution.py:27
  166.7 3.5 %collective-permute-done.31 = f32[6,1,1024]{2,1,0:T(1,128)S(1)} collective-permute-done((f32[6,1,1024]{2,1,0:T(1,128)S(1)}, f32[6,1,1024]{2,1,0:T(1,128)S(1)}, u32[]{:S(2)}, u32[]{:S(2)}) %collective-permute-start.31) | collective-permute-done | bytes 24608 | tf_op jit(solution)/shard_map/ppermute | solution.py:29
  171.9 8.8 %all-reduce.22 = (f32[]{:T(128)}, f32[]{:T(128)}) all-reduce(f32[]{:T(128)} %get-tuple-element.25, f32[]{:T(128)} %get-tuple-element.24), channel_id=1, replica_groups=mesh['gx'=8,'gy'=4] {'gy'}, use_global_device_ids=true, to_apply=%region_9.10 | all-reduce | flops 2 | bytes 16 | tf_op jit(solution)/shard_map/psum | solution.py:13
  180.7 20.4 %all-reduce.18 = (f32[]{:T(128)}, f32[]{:T(128)}) all-reduce(f32[]{:T(128)} %get-tuple-element.40, f32[]{:T(128)} %get-tuple-element.41), channel_id=1, replica_groups=mesh['gx'=8,'gy'=4] {'gx'}, use_global_device_ids=true, to_apply=%region_10.11 | all-reduce | flops 2 | bytes 16 | tf_op jit(solution)/shard_map/psum | solution.py:13
  214.3 4.1 %collective-permute-start.34 = (f32[6,1,1024]{2,1,0:T(1,128)S(1)}, f32[6,1,1024]{2,1,0:T(1,128)S(1)}, u32[]{:S(2)}, u32[]{:S(2)}) collective-permute-start(f32[6,1,1024]{2,1,0:T(1,128)S(1)} %get-tuple-element.62), channel_id=1, source_target_pairs={{0,1},{1,2},{2,3},{4,5},{5,6},{6,7},{8,9},{9,10},{10,11},{12,13},{... | collective-permute-start | bytes 73736 | tf_op jit(solution)/shard_map/ppermute | solution.py:27
  224.6 8.9 %all-reduce.21 = (f32[]{:T(128)}, f32[]{:T(128)}) all-reduce(f32[]{:T(128)} %get-tuple-element.23, f32[]{:T(128)} %get-tuple-element.22), channel_id=1, replica_groups=mesh['gx'=8,'gy'=4] {'gy'}, use_global_device_ids=true, to_apply=%region_15.16 | all-reduce | flops 2 | bytes 16 | tf_op jit(solution)/shard_map/psum | solution.py:13
  233.5 20.8 %all-reduce.17 = (f32[]{:T(128)}, f32[]{:T(128)}) all-reduce(f32[]{:T(128)} %get-tuple-element.38, f32[]{:T(128)} %get-tuple-element.39), channel_id=1, replica_groups=mesh['gx'=8,'gy'=4] {'gx'}, use_global_device_ids=true, to_apply=%region_16.17 | all-reduce | flops 2 | bytes 16 | tf_op jit(solution)/shard_map/psum | solution.py:13
  270.8 3.5 %collective-permute-done.39 = f32[6,1,1024]{2,1,0:T(1,128)S(1)} collective-permute-done((f32[6,1,1024]{2,1,0:T(1,128)S(1)}, f32[6,1,1024]{2,1,0:T(1,128)S(1)}, u32[]{:S(2)}, u32[]{:S(2)}) %collective-permute-start.39) | collective-permute-done | bytes 24608 | tf_op jit(solution)/shard_map/ppermute | solution.py:29
  275.2 8.9 %all-reduce.20 = (f32[]{:T(128)}, f32[]{:T(128)}) all-reduce(f32[]{:T(128)} %get-tuple-element.44, f32[]{:T(128)} %fusion.6), channel_id=1, replica_groups=mesh['gx'=8,'gy'=4] {'gy'}, use_global_device_ids=true, to_apply=%region_21.22 | all-reduce | flops 2 | bytes 16 | tf_op jit(solution)/shard_map/psum | solution.py:13
  284.1 19.5 %all-reduce.16 = (f32[]{:T(128)}, f32[]{:T(128)}) all-reduce(f32[]{:T(128)} %get-tuple-element.36, f32[]{:T(128)} %get-tuple-element.37), channel_id=1, replica_groups=mesh['gx'=8,'gy'=4] {'gx'}, use_global_device_ids=true, to_apply=%region_22.23 | all-reduce | flops 2 | bytes 16 | tf_op jit(solution)/shard_map/psum | solution.py:13
  (221 shorter events, 102.8 us)
Async XLA Ops:
  1.6 43.0 %collective-permute-start = (f32[1,16,1024]{2,1,0:T(8,128)S(1)}, f32[1,16,1024]{2,1,0:T(8,128)S(1)}, u32[]{:S(2)}, u32[]{:S(2)}) collective-permute-start(f32[1,16,1024]{2,1,0:T(8,128)S(1)} %get-tuple-element.120), channel_id=1, source_target_pairs={{0,4},{4,8},{8,12},{12,16},{16,20},{20,24},{24,28},{1,5},{5,9},{9,... | collective-permute-start | bytes 196616 | tf_op jit(solution)/shard_map/ppermute | solution.py:27
  6.5 41.2 %collective-permute-start.1 = (f32[1,16,1024]{2,1,0:T(8,128)S(1)}, f32[1,16,1024]{2,1,0:T(8,128)S(1)}, u32[]{:S(2)}, u32[]{:S(2)}) collective-permute-start(f32[1,16,1024]{2,1,0:T(8,128)S(1)} %get-tuple-element.121), channel_id=1, source_target_pairs={{4,0},{8,4},{12,8},{16,12},{20,16},{24,20},{28,24},{5,1},{9,5},{13... | collective-permute-start | bytes 196616 | tf_op jit(solution)/shard_map/ppermute | solution.py:29
  8.6 43.8 %collective-permute-start.19 = (f32[1,16,1024]{2,1,0:T(8,128)}, f32[1,16,1024]{2,1,0:T(8,128)S(1)}, u32[]{:S(2)}, u32[]{:S(2)}) collective-permute-start(f32[1,16,1024]{2,1,0:T(8,128)} %get-tuple-element.98), channel_id=1, source_target_pairs={{4,0},{8,4},{12,8},{16,12},{20,16},{24,20},{28,24},{5,1},{9,5},{13... | collective-permute-start | bytes 196616 | tf_op jit(solution)/shard_map/ppermute | solution.py:29
  9.9 41.1 %collective-permute-start.17 = (f32[1,16,1024]{2,1,0:T(8,128)S(1)}, f32[1,16,1024]{2,1,0:T(8,128)S(1)}, u32[]{:S(2)}, u32[]{:S(2)}) collective-permute-start(f32[1,16,1024]{2,1,0:T(8,128)S(1)} %get-tuple-element.99), channel_id=1, source_target_pairs={{0,4},{4,8},{8,12},{12,16},{16,20},{20,24},{24,28},{1,5},{5,9},{9,... | collective-permute-start | bytes 196616 | tf_op jit(solution)/shard_map/ppermute | solution.py:27
  15.1 21.3 %collective-permute-start.16 = (f32[1,16,1024]{2,1,0:T(8,128)S(1)}, f32[1,16,1024]{2,1,0:T(8,128)S(1)}, u32[]{:S(2)}, u32[]{:S(2)}) collective-permute-start(f32[1,16,1024]{2,1,0:T(8,128)S(1)} %get-tuple-element.104), channel_id=1, source_target_pairs={{0,4},{4,8},{8,12},{12,16},{16,20},{20,24},{24,28},{1,5},{5,9},{9,... | collective-permute-start | bytes 196616 | tf_op jit(solution)/shard_map/ppermute | solution.py:27
  36.4 6.2 %collective-permute-start.18 = (f32[1,16,1024]{2,1,0:T(8,128)S(1)}, f32[1,16,1024]{2,1,0:T(8,128)S(1)}, u32[]{:S(2)}, u32[]{:S(2)}) collective-permute-start(f32[1,16,1024]{2,1,0:T(8,128)S(1)} %get-tuple-element.105), channel_id=1, source_target_pairs={{4,0},{8,4},{12,8},{16,12},{20,16},{24,20},{28,24},{5,1},{9,5},{13... | collective-permute-start | bytes 196616 | tf_op jit(solution)/shard_map/ppermute | solution.py:29
  43.3 57.0 %collective-permute-start.22 = (f32[6,1,1024]{2,1,0:T(1,128)}, f32[6,1,1024]{2,1,0:T(1,128)S(1)}, u32[]{:S(2)}, u32[]{:S(2)}) collective-permute-start(f32[6,1,1024]{2,1,0:T(1,128)} %get-tuple-element.68), channel_id=1, source_target_pairs={{1,0},{2,1},{3,2},{5,4},{6,5},{7,6},{9,8},{10,9},{11,10},{13,12},{... | collective-permute-start | bytes 73736 | tf_op jit(solution)/shard_map/ppermute | solution.py:29
  44.6 55.7 %collective-permute-start.20 = (f32[6,1,1024]{2,1,0:T(1,128)}, f32[6,1,1024]{2,1,0:T(1,128)S(1)}, u32[]{:S(2)}, u32[]{:S(2)}) collective-permute-start(f32[6,1,1024]{2,1,0:T(1,128)} %get-tuple-element.69), channel_id=1, source_target_pairs={{0,1},{1,2},{2,3},{4,5},{5,6},{6,7},{8,9},{9,10},{10,11},{12,13},{... | collective-permute-start | bytes 73736 | tf_op jit(solution)/shard_map/ppermute | solution.py:27
  47.8 9.0 %collective-permute-start.2 = (f32[6,1,1024]{2,1,0:T(1,128)S(1)}, f32[6,1,1024]{2,1,0:T(1,128)S(1)}, u32[]{:S(2)}, u32[]{:S(2)}) collective-permute-start(f32[6,1,1024]{2,1,0:T(1,128)S(1)} %get-tuple-element.78), channel_id=1, source_target_pairs={{0,1},{1,2},{2,3},{4,5},{5,6},{6,7},{8,9},{9,10},{10,11},{12,13},{... | collective-permute-start | bytes 73736 | tf_op jit(solution)/shard_map/ppermute | solution.py:27
  53.8 46.6 %collective-permute-start.21 = (f32[6,1,1024]{2,1,0:T(1,128)}, f32[6,1,1024]{2,1,0:T(1,128)S(1)}, u32[]{:S(2)}, u32[]{:S(2)}) collective-permute-start(f32[6,1,1024]{2,1,0:T(1,128)} %get-tuple-element.70), channel_id=1, source_target_pairs={{0,1},{1,2},{2,3},{4,5},{5,6},{6,7},{8,9},{9,10},{10,11},{12,13},{... | collective-permute-start | bytes 73736 | tf_op jit(solution)/shard_map/ppermute | solution.py:27
  57.3 6.2 %collective-permute-start.4 = (f32[1,16,1024]{2,1,0:T(8,128)S(1)}, f32[1,16,1024]{2,1,0:T(8,128)S(1)}, u32[]{:S(2)}, u32[]{:S(2)}) collective-permute-start(f32[1,16,1024]{2,1,0:T(8,128)S(1)} %get-tuple-element.116), channel_id=1, source_target_pairs={{0,4},{4,8},{8,12},{12,16},{16,20},{20,24},{24,28},{1,5},{5,9},{9,... | collective-permute-start | bytes 196616 | tf_op jit(solution)/shard_map/ppermute | solution.py:27
  61.6 6.4 %collective-permute-start.5 = (f32[1,16,1024]{2,1,0:T(8,128)S(1)}, f32[1,16,1024]{2,1,0:T(8,128)S(1)}, u32[]{:S(2)}, u32[]{:S(2)}) collective-permute-start(f32[1,16,1024]{2,1,0:T(8,128)S(1)} %get-tuple-element.117), channel_id=1, source_target_pairs={{4,0},{8,4},{12,8},{16,12},{20,16},{24,20},{28,24},{5,1},{9,5},{13... | collective-permute-start | bytes 196616 | tf_op jit(solution)/shard_map/ppermute | solution.py:29
  77.9 6.2 %collective-permute-start.9 = (f32[1,16,1024]{2,1,0:T(8,128)S(1)}, f32[1,16,1024]{2,1,0:T(8,128)S(1)}, u32[]{:S(2)}, u32[]{:S(2)}) collective-permute-start(f32[1,16,1024]{2,1,0:T(8,128)S(1)} %get-tuple-element.113), channel_id=1, source_target_pairs={{4,0},{8,4},{12,8},{16,12},{20,16},{24,20},{28,24},{5,1},{9,5},{13... | collective-permute-start | bytes 196616 | tf_op jit(solution)/shard_map/ppermute | solution.py:29
  88.5 11.9 %collective-permute-start.23 = (f32[6,1,1024]{2,1,0:T(1,128)}, f32[6,1,1024]{2,1,0:T(1,128)S(1)}, u32[]{:S(2)}, u32[]{:S(2)}) collective-permute-start(f32[6,1,1024]{2,1,0:T(1,128)} %get-tuple-element.71), channel_id=1, source_target_pairs={{1,0},{2,1},{3,2},{5,4},{6,5},{7,6},{9,8},{10,9},{11,10},{13,12},{... | collective-permute-start | bytes 73736 | tf_op jit(solution)/shard_map/ppermute | solution.py:29
  103.9 6.5 %collective-permute-start.24 = (f32[1,16,1024]{2,1,0:T(8,128)S(1)}, f32[1,16,1024]{2,1,0:T(8,128)S(1)}, u32[]{:S(2)}, u32[]{:S(2)}) collective-permute-start(f32[1,16,1024]{2,1,0:T(8,128)S(1)} %get-tuple-element.92), channel_id=1, source_target_pairs={{0,4},{4,8},{8,12},{12,16},{16,20},{20,24},{24,28},{1,5},{5,9},{9,... | collective-permute-start | bytes 196616 | tf_op jit(solution)/shard_map/ppermute | solution.py:27
  108.2 6.2 %collective-permute-start.25 = (f32[1,16,1024]{2,1,0:T(8,128)S(1)}, f32[1,16,1024]{2,1,0:T(8,128)S(1)}, u32[]{:S(2)}, u32[]{:S(2)}) collective-permute-start(f32[1,16,1024]{2,1,0:T(8,128)S(1)} %get-tuple-element.93), channel_id=1, source_target_pairs={{4,0},{8,4},{12,8},{16,12},{20,16},{24,20},{28,24},{5,1},{9,5},{13... | collective-permute-start | bytes 196616 | tf_op jit(solution)/shard_map/ppermute | solution.py:29
  152.9 10.8 %collective-permute-start.28 = (f32[1,16,1024]{2,1,0:T(8,128)S(1)}, f32[1,16,1024]{2,1,0:T(8,128)S(1)}, u32[]{:S(2)}, u32[]{:S(2)}) collective-permute-start(f32[1,16,1024]{2,1,0:T(8,128)S(1)} %get-tuple-element.88), channel_id=1, source_target_pairs={{0,4},{4,8},{8,12},{12,16},{16,20},{20,24},{24,28},{1,5},{5,9},{9,... | collective-permute-start | bytes 196616 | tf_op jit(solution)/shard_map/ppermute | solution.py:27
  155.3 8.4 %collective-permute-start.29 = (f32[1,16,1024]{2,1,0:T(8,128)S(1)}, f32[1,16,1024]{2,1,0:T(8,128)S(1)}, u32[]{:S(2)}, u32[]{:S(2)}) collective-permute-start(f32[1,16,1024]{2,1,0:T(8,128)S(1)} %get-tuple-element.89), channel_id=1, source_target_pairs={{4,0},{8,4},{12,8},{16,12},{20,16},{24,20},{28,24},{5,1},{9,5},{13... | collective-permute-start | bytes 196616 | tf_op jit(solution)/shard_map/ppermute | solution.py:29
  157.3 52.1 %collective-permute-start.12 = (f32[1,16,1024]{2,1,0:T(8,128)}, f32[1,16,1024]{2,1,0:T(8,128)}, u32[]{:S(2)}, u32[]{:S(2)}) collective-permute-start(f32[1,16,1024]{2,1,0:T(8,128)} %get-tuple-element.108), channel_id=1, source_target_pairs={{0,4},{4,8},{8,12},{12,16},{16,20},{20,24},{24,28},{1,5},{5,9},{9,... | collective-permute-start | bytes 196616 | tf_op jit(solution)/shard_map/ppermute | solution.py:27
  162.5 47.0 %collective-permute-start.13 = (f32[1,16,1024]{2,1,0:T(8,128)}, f32[1,16,1024]{2,1,0:T(8,128)}, u32[]{:S(2)}, u32[]{:S(2)}) collective-permute-start(f32[1,16,1024]{2,1,0:T(8,128)} %get-tuple-element.109), channel_id=1, source_target_pairs={{4,0},{8,4},{12,8},{16,12},{20,16},{24,20},{28,24},{5,1},{9,5},{13... | collective-permute-start | bytes 196616 | tf_op jit(solution)/shard_map/ppermute | solution.py:29
  206.8 7.2 %collective-permute-start.32 = (f32[1,16,1024]{2,1,0:T(8,128)S(1)}, f32[1,16,1024]{2,1,0:T(8,128)S(1)}, u32[]{:S(2)}, u32[]{:S(2)}) collective-permute-start(f32[1,16,1024]{2,1,0:T(8,128)S(1)} %get-tuple-element.84), channel_id=1, source_target_pairs={{0,4},{4,8},{8,12},{12,16},{16,20},{20,24},{24,28},{1,5},{5,9},{9,... | collective-permute-start | bytes 196616 | tf_op jit(solution)/shard_map/ppermute | solution.py:27
  208.1 6.2 %collective-permute-start.33 = (f32[1,16,1024]{2,1,0:T(8,128)S(1)}, f32[1,16,1024]{2,1,0:T(8,128)S(1)}, u32[]{:S(2)}, u32[]{:S(2)}) collective-permute-start(f32[1,16,1024]{2,1,0:T(8,128)S(1)} %get-tuple-element.85), channel_id=1, source_target_pairs={{4,0},{8,4},{12,8},{16,12},{20,16},{24,20},{28,24},{5,1},{9,5},{13... | collective-permute-start | bytes 196616 | tf_op jit(solution)/shard_map/ppermute | solution.py:29
  210.9 52.0 %collective-permute-start.14 = (f32[6,1,1024]{2,1,0:T(1,128)}, f32[6,1,1024]{2,1,0:T(1,128)}, u32[]{:S(2)}, u32[]{:S(2)}) collective-permute-start(f32[6,1,1024]{2,1,0:T(1,128)} %get-tuple-element.72), channel_id=1, source_target_pairs={{0,1},{1,2},{2,3},{4,5},{5,6},{6,7},{8,9},{9,10},{10,11},{12,13},{... | collective-permute-start | bytes 73736 | tf_op jit(solution)/shard_map/ppermute | solution.py:27
  212.8 50.2 %collective-permute-start.15 = (f32[6,1,1024]{2,1,0:T(1,128)}, f32[6,1,1024]{2,1,0:T(1,128)}, u32[]{:S(2)}, u32[]{:S(2)}) collective-permute-start(f32[6,1,1024]{2,1,0:T(1,128)} %get-tuple-element.73), channel_id=1, source_target_pairs={{1,0},{2,1},{3,2},{5,4},{6,5},{7,6},{9,8},{10,9},{11,10},{13,12},{... | collective-permute-start | bytes 73736 | tf_op jit(solution)/shard_map/ppermute | solution.py:29
  (56 other events, 504.1 us)
